TPU v7x, 128 devices: a whole 4x4x4 slice. The times are simulated.
128 devices in a mesh: lat: 4 (over x), ord: 16 (over y, z), batch: 2 (over core).
Axes of the slice: x: 4, y: 4, z: 4, core: 2. Of those that a mesh axis runs over, the one named last changes fastest.
Arguments:
- state_field: bfloat16 [512, 720, 1440], P(('batch', 'ord'), 'lat'), parts along dimension 0, may hold values from -6 to 6
- slot_order: int32 [512], replicated, may hold values from 0 to 511, each once
- legendre: bfloat16 [512, 720, 720], P(('lat', 'ord')), may hold values from -0.21875 to 0.21875
- degree_gain: float32 [720, 256], replicated, may hold values from 0.25 to 1.75
- mixing: bfloat16 [256, 256], replicated, may hold values from -0.375 to 0.375
Outputs:
- updated: bfloat16 [512, 720, 1440], P(('batch', 'ord'), 'lat'), parts along dimension 0
There are 2 independent parts, one for each index of `batch`. A program takes and returns all parts, laid end to end along the dimension named above; an argument that names none is the same for every part. Nothing has to cross between parts.
Inputs may be any that keep to these rules, and one draw needn't show every extreme that they name: `slot_order`: each of 0 to 511 stands once.
All inputs are finite; a program needn't handle non-finite values.
Results may differ from a plain program's by a relative error of at most 0.0054.
Values may be sent and summed in bfloat16 or wider, within the bound.
A program may use at most 192 MiB of HBM per device.

v0:
```python
import math
import jax
import jax.numpy as jnp
from jax import lax
from jax.sharding import PartitionSpec as P


def tables(orders, lon_count):
    longitude = jnp.arange(lon_count, dtype=jnp.int32)
    phase = orders[:, None] * longitude[None, :] % lon_count
    angle = phase.astype(jnp.float32) * (2.0 * math.pi / lon_count)
    root = 1.0 / math.sqrt(lon_count)
    cosine = jnp.cos(angle)
    sine = jnp.sin(angle)
    forward = jnp.stack([cosine * root, -sine * root], axis=1).astype(jnp.bfloat16)
    weights = jnp.where(orders == 0, 1.0, 2.0).astype(jnp.float32) * root
    inverse = jnp.stack([cosine * weights[:, None], -sine * weights[:, None]], axis=1).astype(
        jnp.bfloat16
    )
    return (forward, inverse)


def shards(state_field, slot_order, legendre, degree_gain, mixing):
    channels, lat_rows, lon_count = state_field.shape
    all_slots = slot_order.shape[0]
    my_slots, degrees, latitudes = legendre.shape
    width = mixing.shape[0]
    lat_count = lax.axis_size("lat")
    ord_count = lax.axis_size("ord")
    forward, inverse = tables(slot_order, lon_count)
    fourier = lax.dot_general(
        forward.reshape(2 * all_slots, lon_count),
        state_field.reshape(channels * lat_rows, lon_count),
        (((1,), (1,)), ((), ())),
        preferred_element_type=jnp.float32,
    )
    fourier = fourier.astype(jnp.bfloat16)
    arrived = lax.all_to_all(
        fourier.reshape(1, all_slots, 2, channels, lat_rows),
        ("lat", "ord"),
        split_axis=1,
        concat_axis=0,
        tiled=True,
    )
    arrived = arrived.reshape(lat_count, ord_count, my_slots, 2, channels, lat_rows).transpose(
        2, 3, 1, 4, 0, 5
    )
    gathered = arrived.reshape(my_slots, 2 * width, latitudes)
    orders_here = lax.dynamic_slice_in_dim(
        slot_order, lax.axis_index(("lat", "ord")) * my_slots, my_slots, 0
    )
    padded_gain = jnp.concatenate([degree_gain, jnp.zeros((degrees, width), jnp.float32)], axis=0)
    spec = jnp.einsum("sjl,sxl->sjx", legendre, gathered, preferred_element_type=jnp.float32)

    def pick_rows(order_value):
        return lax.dynamic_slice_in_dim(padded_gain, order_value, degrees, 0)

    gain_rows = jax.vmap(pick_rows)(orders_here)
    kept = jnp.arange(degrees, dtype=jnp.int32)[None, :] < (degrees - orders_here)[:, None]
    filtered = jnp.where(
        kept[:, :, None, None],
        spec.reshape(my_slots, degrees, 2, width) * gain_rows[:, :, None, :],
        0.0,
    )
    filtered = filtered.astype(jnp.bfloat16)
    mixed = jnp.dot(
        filtered.reshape(my_slots * degrees * 2, width), mixing, preferred_element_type=jnp.float32
    )
    mixed = mixed.astype(jnp.bfloat16).reshape(my_slots, degrees, 2 * width)
    synth = jnp.einsum("sjx,sjl->sxl", mixed, legendre, preferred_element_type=jnp.float32).astype(
        jnp.bfloat16
    )
    outgoing = synth.reshape(my_slots, 2, ord_count, channels, lat_count, lat_rows).transpose(
        4, 2, 0, 1, 3, 5
    )
    outgoing = outgoing.reshape(lat_count * ord_count, my_slots, 2, channels, lat_rows)
    returned = lax.all_to_all(outgoing, ("lat", "ord"), split_axis=0, concat_axis=0, tiled=True)
    returned = returned.reshape(2 * all_slots, channels * lat_rows)
    back = lax.dot_general(
        returned,
        inverse.reshape(2 * all_slots, lon_count),
        (((0,), (0,)), ((), ())),
        preferred_element_type=jnp.float32,
    )
    back = back.reshape(channels, lat_rows, lon_count)
    return (state_field.astype(jnp.float32) + jax.nn.gelu(back, approximate=True)).astype(
        jnp.bfloat16
    )


def solution(mesh):
    placed = (P(("batch", "ord"), "lat", None), P(), P(("lat", "ord"), None, None), P(), P())
    return jax.shard_map(
        shards,
        mesh=mesh,
        in_specs=placed,
        out_specs=P(("batch", "ord"), "lat", None),
        check_vma=False,
    )
```

profile of v0, /device:TPU:82, one launch (start us, length us, event | category | flops | bytes accessed | tf_op | source)
XLA Modules:
  0.0 555.3 jit_solution(5158348730062671081)
XLA Ops:
  0.7 14.0 %multiply_convert_fusion.1 = (bf16[512,1,1440]{0,2,1:T(8,128)(2,1)S(1)}, bf16[512,1,1440]{0,2,1:T(8,128)(2,1)S(1)}, bf16[512,1,1440]{0,2,1:T(8,128)(2,1)S(1)}, bf16[512,1,1440]{0,2,1:T(8,128)(2,1)S(1)}) fusion(f32[512]{0:T(512)S(1)} %select_multiply_fusion, s32[512]{0:T(512)} %param.6), kind=kLoop, calls=%fused_computation.28 | loop fusion | flops 13271040 | bytes 5902336 | tf_op jit(solution)/shard_map/convert
  28.6 11.9 %copy.34 = bf16[16,180,1440]{2,1,0:T(8,128)(2,1)} copy(bf16[16,180,1440]{2,0,1:T(8,128)(2,1)} %param.5) | data formatting | bytes 16588800 | tf_op args[0]
  40.5 10.9 %reshape.240 = bf16[2880,1440]{1,0:T(8,128)(2,1)} reshape(bf16[16,180,1440]{2,1,0:T(8,128)(2,1)} %copy.34) | data formatting | bytes 16588800 | tf_op jit(solution)/shard_map/reshape | solution.py:33
  51.4 13.7 %convolution_convert_fusion.1 = bf16[1024,2880]{0,1:T(8,128)(2,1)} fusion(bf16[1024,1440]{1,0:T(8,128)(2,1)S(1)} %copy-done.2, bf16[2880,1440]{1,0:T(8,128)(2,1)} %reshape.240), kind=kOutput, calls=%fused_computation.17 | convolution fusion | flops 8496414720 | bytes 17141760 | tf_op jit(solution)/shard_map/dot_general | solution.py:31
  65.1 8.5 %copy.35 = bf16[1024,2880]{1,0:T(8,128)(2,1)} copy(bf16[1024,2880]{0,1:T(8,128)(2,1)} %convolution_convert_fusion.1) | data formatting | bytes 11796480 | tf_op jit(solution)/shard_map/convert_element_type | solution.py:37
  73.6 27.5 %reshape.241 = bf16[1,512,2,16,180]{4,3,2,1,0:T(8,128)(2,1)} reshape(bf16[1024,2880]{1,0:T(8,128)(2,1)} %copy.35) | data formatting | bytes 11796480 | tf_op jit(solution)/shard_map/reshape | solution.py:39
  101.1 11.5 %all-to-all-start = ((bf16[1,512,2,16,180]{4,3,2,0,1:T(8,128)(2,1)}), bf16[1,512,2,16,180]{4,3,2,0,1:T(8,128)(2,1)}, u32[]{:S(2)}, u32[]{:S(2)}) async-start(bf16[1,512,2,16,180]{4,3,2,0,1:T(8,128)(2,1)} %bitcast.34), calls=%async_computation | async-start | bytes 16777216 | tf_op jit(solution)/shard_map/all_to_all | solution.py:38
  113.4 17.8 %while.1 = (s32[]{:T(128)}, f32[1440,256]{1,0:T(8,128)S(1)}, s32[8,2]{0,1:T(2,128)S(1)}, f32[8,720,256]{2,1,0:T(8,128)}, s32[]{:T(128)}) while((s32[]{:T(128)}, f32[1440,256]{1,0:T(8,128)S(1)}, s32[8,2]{0,1:T(2,128)S(1)}, f32[8,720,256]{2,1,0:T(8,128)}, s32[]{:T(128)}) %tuple.21), condition=%wide.while_cond, body=%wide.while_body.sunk | while | flops 2 | bytes 1475173 | solution.py:56
  131.3 13.0 %mul.158 = f32[8,720,2,256]{3,2,1,0:T(2,128)} broadcast(f32[8,720,256]{2,1,0:T(8,128)} %get-tuple-element.12), dimensions={0,1,3} | broadcast | bytes 17694720 | tf_op jit(solution)/shard_map/mul | solution.py:62
  144.3 14.9 %mul.159 = f32[11520,256]{1,0:T(8,128)} reshape(f32[8,720,2,256]{3,2,1,0:T(2,128)} %mul.158) | data formatting | bytes 23592960 | tf_op jit(solution)/shard_map/mul | solution.py:62
  163.2 71.0 %all-to-all-done = bf16[1,512,2,16,180]{4,3,2,0,1:T(8,128)(2,1)} async-done(((bf16[1,512,2,16,180]{4,3,2,0,1:T(8,128)(2,1)}), bf16[1,512,2,16,180]{4,3,2,0,1:T(8,128)(2,1)}, u32[]{:S(2)}, u32[]{:S(2)}) %all-to-all-start) | async-done | bytes 5898272 | tf_op jit(solution)/shard_map/all_to_all | solution.py:38
  234.1 12.1 %copy.56 = bf16[4,16,8,2,16,180]{5,0,4,1,3,2:T(4,128)(2,1)} copy(bf16[4,16,8,2,16,180]{5,4,3,2,1,0:T(8,128)(2,1)} %bitcast.1) | data formatting | bytes 11796480 | tf_op jit(solution)/shard_map/reshape | solution.py:45
  246.3 15.3 %reshape.243 = bf16[8,512,720]{2,1,0:T(8,128)(2,1)} reshape(bf16[8,2,16,16,4,180]{5,4,3,2,1,0:T(4,128)(2,1)} %bitcast.35) | data formatting | bytes 11796480 | tf_op jit(solution)/shard_map/reshape | solution.py:48
  261.5 14.4 %convolution_bitcast_fusion = f32[8,720,512]{2,1,0:T(8,128)} fusion(bf16[8,512,720]{2,1,0:T(8,128)(2,1)} %reshape.243, bf16[8,720,720]{2,1,0:T(8,128)(2,1)} %param.7), kind=kOutput, calls=%fused_computation.19 | convolution fusion | flops 4246732800 | bytes 25989120 | tf_op jit(solution)/shard_map/sjl,sxl->sjx/dot_general | solution.py:53
  276.0 13.5 %reshape.244 = f32[11520,256]{1,0:T(8,128)} reshape(f32[8,720,512]{2,1,0:T(8,128)} %convolution_bitcast_fusion) | data formatting | bytes 23592960 | tf_op jit(solution)/shard_map/reshape | solution.py:62
  289.5 13.4 %convolution_convert_fusion = bf16[11520,256]{1,0:T(8,128)(2,1)} fusion(bf16[256,256]{1,0:T(8,128)(2,1)S(1)} %copy-done, f32[11520,256]{1,0:T(8,128)} %reshape.244, f32[11520,256]{1,0:T(8,128)} %mul.159, pred[11520]{0:T(1024)(128)(4,1)S(1)} %broadcast_in_dim.37), kind=kOutput, calls=%fused_computation.12 | convolution fusion | flops 1521745920 | bytes 29633792 | tf_op jit(solution)/shard_map/dot_general | solution.py:66
  302.9 9.7 %reshape.245 = bf16[8,720,512]{2,1,0:T(8,128)(2,1)} reshape(bf16[11520,256]{1,0:T(8,128)(2,1)} %convolution_convert_fusion) | data formatting | bytes 11796480 | tf_op jit(solution)/shard_map/reshape | solution.py:69
  312.6 11.8 %convolution_convert_fusion.2 = bf16[8,512,720]{1,2,0:T(8,128)(2,1)} fusion(bf16[8,720,512]{2,1,0:T(8,128)(2,1)} %reshape.245, bf16[8,720,720]{2,1,0:T(8,128)(2,1)} %param.7), kind=kOutput, calls=%fused_computation.20 | convolution fusion | flops 4249681920 | bytes 20090880 | tf_op jit(solution)/shard_map/sjx,sjl->sxl/dot_general | solution.py:70
  332.9 18.0 %reshape.246 = bf16[8,2,16,16,4,180]{5,4,3,2,1,0:T(4,128)(2,1)} reshape(bf16[8,512,720]{2,1,0:T(8,128)(2,1)} %copy.40) | data formatting | bytes 11796480 | tf_op jit(solution)/shard_map/reshape | solution.py:73
  359.2 9.6 %all-to-all-start.1 = ((bf16[64,8,2,16,180]{4,3,2,1,0:T(8,128)(2,1)}), bf16[64,8,2,16,180]{4,3,2,1,0:T(8,128)(2,1)}, u32[]{:S(2)}, u32[]{:S(2)}) async-start(bf16[64,8,2,16,180]{4,3,2,1,0:T(8,128)(2,1)} %bitcast.37), calls=%async_computation.1 | async-start | bytes 16777216 | tf_op jit(solution)/shard_map/all_to_all | solution.py:77
  379.7 111.8 %all-to-all-done.1 = bf16[64,8,2,16,180]{4,3,2,1,0:T(8,128)(2,1)} async-done(((bf16[64,8,2,16,180]{4,3,2,1,0:T(8,128)(2,1)}), bf16[64,8,2,16,180]{4,3,2,1,0:T(8,128)(2,1)}, u32[]{:S(2)}, u32[]{:S(2)}) %all-to-all-start.1) | async-done | bytes 5898272 | tf_op jit(solution)/shard_map/all_to_all | solution.py:77
  491.5 15.6 %reshape.248 = bf16[1024,2880]{1,0:T(8,128)(2,1)} reshape(bf16[64,8,2,16,180]{4,3,2,1,0:T(8,128)(2,1)} %all-to-all-done.1) | data formatting | bytes 11796480 | tf_op jit(solution)/shard_map/reshape | solution.py:78
  523.5 16.3 %fusion.11 = f32[16,180,1440]{2,1,0:T(8,128)} fusion(bf16[16,180,1024]{2,1,0:T(8,128)(2,1)} %dot_general.27, bf16[1024,1440]{1,0:T(8,128)(2,1)} %convert_element_type.70), kind=kOutput, calls=%fused_computation.21 | convolution fusion | flops 8493465600 | bytes 25436160 | tf_op jit(solution)/shard_map/dot_general | solution.py:79
  539.8 15.3 %fusion.8 = bf16[16,180,1440]{2,0,1:T(8,128)(2,1)} fusion(f32[16,180,1440]{2,1,0:T(8,128)} %fusion.11, bf16[16,180,1440]{2,0,1:T(8,128)(2,1)S(1)} %bitcast.33), kind=kLoop, calls=%fused_computation.11 | loop fusion | flops 45619200 | bytes 33177600 | tf_op jit(solution)/shard_map/convert_element_type | solution.py:86
  (56 shorter events, 81.4 us)
Async XLA Ops:
  0.0 289.5 %copy-start = (bf16[256,256]{1,0:T(8,128)(2,1)S(1)}, bf16[256,256]{1,0:T(8,128)(2,1)}, u32[]{:S(2)}) copy-start(bf16[256,256]{1,0:T(8,128)(2,1)} %param.9) | copy-start | bytes 393220
  40.5 10.9 %copy-start.2 = (bf16[1024,1440]{1,0:T(8,128)(2,1)S(1)}, bf16[1024,1440]{1,0:T(8,128)(2,1)}, u32[]{:S(2)}) copy-start(bf16[1024,1440]{1,0:T(8,128)(2,1)} %convert_element_type.65) | copy-start | bytes 8847364
  101.1 12.3 %copy-start.3 = (f32[720,256]{1,0:T(8,128)S(1)}, f32[720,256]{1,0:T(8,128)}, u32[]{:S(2)}) copy-start(f32[720,256]{1,0:T(8,128)} %param.8) | copy-start | bytes 2211844
  101.1 133.1 %all-to-all-start = ((bf16[1,512,2,16,180]{4,3,2,0,1:T(8,128)(2,1)}), bf16[1,512,2,16,180]{4,3,2,0,1:T(8,128)(2,1)}, u32[]{:S(2)}, u32[]{:S(2)}) async-start(bf16[1,512,2,16,180]{4,3,2,0,1:T(8,128)(2,1)} %bitcast.34), calls=%async_computation | async-start | bytes 16777216 | tf_op jit(solution)/shard_map/all_to_all | solution.py:38
  359.2 132.4 %all-to-all-start.1 = ((bf16[64,8,2,16,180]{4,3,2,1,0:T(8,128)(2,1)}), bf16[64,8,2,16,180]{4,3,2,1,0:T(8,128)(2,1)}, u32[]{:S(2)}, u32[]{:S(2)}) async-start(bf16[64,8,2,16,180]{4,3,2,1,0:T(8,128)(2,1)} %bitcast.37), calls=%async_computation.1 | async-start | bytes 16777216 | tf_op jit(solution)/shard_map/all_to_all | solution.py:77
  515.5 24.3 %slice-start = ((s8[8847360]{0:T(1024)(128)(4,1)}), s8[458752]{0:T(1024)(128)(4,1)S(1)}, s32[]{:S(2)}) async-start(s8[8847360]{0:T(1024)(128)(4,1)} %bitcast.32), calls=%async_computation.2 | async-start | bytes 917504
  523.5 16.3 %slice-start.1 = ((s8[8847360]{0:T(1024)(128)(4,1)}), s8[4194304]{0:T(1024)(128)(4,1)S(1)}, s32[]{:S(2)}) async-start(s8[8847360]{0:T(1024)(128)(4,1)} %bitcast.32), calls=%async_computation.3 | async-start | bytes 8388608
  523.5 16.3 %slice-start.2 = ((s8[8847360]{0:T(1024)(128)(4,1)}), s8[4194304]{0:T(1024)(128)(4,1)S(1)}, s32[]{:S(2)}) async-start(s8[8847360]{0:T(1024)(128)(4,1)} %bitcast.32), calls=%async_computation.4 | async-start | bytes 8388608
  539.8 15.3 %copy-start.1 = (bf16[256,256]{1,0:T(8,128)(2,1)S(1)}, bf16[256,256]{1,0:T(8,128)(2,1)}, u32[]{:S(2)}) copy-start(bf16[256,256]{1,0:T(8,128)(2,1)} %param.9) | copy-start | bytes 393220
where the time goes:
time: 565 us; the launch traced here: 555 us
  local copies, waits for them, and re-layouts  248 us (44%)
  waiting for transfers between devices  183 us (32%)
  matrix products  69.6 us (12%)
  other arithmetic  33.7 us (6%)
  starting transfers between devices  21 us (4%)
    all_to_all x1, waiting for transfers between devices, shards(): lax.all_to_all(outgoing, ('lat', 'ord'), split_axis=0, concat_axis=0, til...  112 us
    all_to_all x1, waiting for transfers between devices, shards(): lax.all_to_all(fourier.reshape(1, all_slots, 2, channels, lat_rows), ('la...  71 us
    mul x2, local copies, waits for them, and re-layouts, shards(): spec.reshape(my_slots, degrees, 2, width) * gain_rows[:, :, None, :]  27.9 us
    reshape x1, local copies, waits for them, and re-layouts, shards(): fourier.reshape(1, all_slots, 2, channels, lat_rows)  27.5 us
    reshape x1, local copies, waits for them, and re-layouts, shards(): synth.reshape(my_slots, 2, ord_count, channels, lat_count, lat_rows)  18 us
    gather x24, local copies, waits for them, and re-layouts  17.8 us
    dot_general x2, local copies, waits for them, and re-layouts, shards(): lax.dot_general(returned, inverse.reshape(2 * all_slots, lon_count), (((0...  16.4 us
    dot_general x1, matrix products, shards(): lax.dot_general(returned, inverse.reshape(2 * all_slots, lon_count), (((0...  16.3 us
  transfers between devices with their start and end apart: 2, of which 2 were waited for; matrix products, arithmetic and copies ran while one was open for 11% of the time, Pallas kernels for 0%

commit v1 on v0

--- a/solution.py
+++ b/solution.py
@@ -35,12 +35,20 @@
         preferred_element_type=jnp.float32,
     )
     fourier = fourier.astype(jnp.bfloat16)
-    arrived = lax.all_to_all(
-        fourier.reshape(1, all_slots, 2, channels, lat_rows),
-        ("lat", "ord"),
-        split_axis=1,
-        concat_axis=0,
-        tiled=True,
+    arrived = jnp.concatenate(
+        lax.all_to_all(
+            jnp.stack(
+                jnp.split(
+                    fourier.reshape(1, all_slots, 2, channels, lat_rows),
+                    lax.axis_size(("lat", "ord")),
+                    1,
+                )
+            ),
+            ("lat", "ord"),
+            0,
+            0,
+        ),
+        0,
     )
     arrived = arrived.reshape(lat_count, ord_count, my_slots, 2, channels, lat_rows).transpose(
         2, 3, 1, 4, 0, 5

time: 565 us -> 667 us (1.18)
  local copies, waits for them, and re-layouts: 248 us -> 346 us
    unnamed x15 -> x78, local copies, waits for them, and re-layouts: 11.9 us -> 110 us
    another operation x0 -> x2, local copies, waits for them, and re-layouts: none -> 13.7 us  [the longest x1 12.1 us: shards(): arrived.reshape(lat_count, ord_count, my_slots, 2, channels, lat_rows)]
    reshape x1 -> x0, local copies, waits for them, and re-layouts: 12.1 us -> none  [shards(): arrived.reshape(lat_count, ord_count, my_slots, 2, channels, lat_rows)]
  transfers between devices with their start and end apart: 2 -> 2, of which waited for: 2 -> 2; matrix products, arithmetic and copies ran while one was open for 11% -> 9% of each run, Pallas kernels for 0% -> 0%
where the time goes in v1:
time: 667 us; the launch traced here: 655 us
  local copies, waits for them, and re-layouts  346 us (52%)
  waiting for transfers between devices  184 us (28%)
  matrix products  69.9 us (10%)
  other arithmetic  33.7 us (5%)
  starting transfers between devices  20.7 us (3%)
    all_to_all x1, waiting for transfers between devices, shards(): lax.all_to_all(outgoing, ('lat', 'ord'), split_axis=0, concat_axis=0, til...  112 us
    unnamed x78, local copies, waits for them, and re-layouts  110 us
    all_to_all x1, waiting for transfers between devices, shards(): lax.all_to_all(jnp.stack(jnp.split(fourier.reshape(1, all_slots, 2, chann...  72.6 us
    mul x2, local copies, waits for them, and re-layouts, shards(): spec.reshape(my_slots, degrees, 2, width) * gain_rows[:, :, None, :]  27.9 us
    reshape x1, local copies, waits for them, and re-layouts, shards(): fourier.reshape(1, all_slots, 2, channels, lat_rows)  27.5 us
    reshape x1, local copies, waits for them, and re-layouts, shards(): synth.reshape(my_slots, 2, ord_count, channels, lat_count, lat_rows)  18 us
    dot_general x2, local copies, waits for them, and re-layouts, shards(): lax.dot_general(returned, inverse.reshape(2 * all_slots, lon_count), (((0...  16.4 us
    dot_general x1, matrix products, shards(): lax.dot_general(returned, inverse.reshape(2 * all_slots, lon_count), (((0...  16.3 us
  transfers between devices with their start and end apart: 2, of which 2 were waited for; matrix products, arithmetic and copies ran while one was open for 9% of the time, Pallas kernels for 0%

profile of v1, /device:TPU:82, one launch (start us, length us, event | category | flops | bytes accessed | tf_op | source)
XLA Modules:
  0.0 655.4 jit_solution(2153268841787886195)
XLA Ops:
  0.7 14.0 %multiply_convert_fusion.1 = (bf16[512,1,1440]{0,2,1:T(8,128)(2,1)S(1)}, bf16[512,1,1440]{0,2,1:T(8,128)(2,1)S(1)}, bf16[512,1,1440]{0,2,1:T(8,128)(2,1)S(1)}, bf16[512,1,1440]{0,2,1:T(8,128)(2,1)S(1)}) fusion(f32[512]{0:T(512)S(1)} %select_multiply_fusion, s32[512]{0:T(512)} %param.6), kind=kLoop, calls=%fused_computation.28 | loop fusion | flops 13271040 | bytes 5902336 | tf_op jit(solution)/shard_map/convert
  28.6 11.9 %copy.22 = bf16[16,180,1440]{2,1,0:T(8,128)(2,1)} copy(bf16[16,180,1440]{2,0,1:T(8,128)(2,1)} %param.5) | data formatting | bytes 16588800 | tf_op args[0]
  40.5 10.9 %reshape.233 = bf16[2880,1440]{1,0:T(8,128)(2,1)} reshape(bf16[16,180,1440]{2,1,0:T(8,128)(2,1)} %copy.22) | data formatting | bytes 16588800 | tf_op jit(solution)/shard_map/reshape | solution.py:33
  51.4 13.9 %convolution_convert_fusion.1 = bf16[1024,2880]{0,1:T(8,128)(2,1)} fusion(bf16[1024,1440]{1,0:T(8,128)(2,1)S(1)} %copy-done.2, bf16[2880,1440]{1,0:T(8,128)(2,1)} %reshape.233), kind=kOutput, calls=%fused_computation.17 | convolution fusion | flops 8496414720 | bytes 17141760 | tf_op jit(solution)/shard_map/dot_general | solution.py:31
  65.3 8.5 %copy.23 = bf16[1024,2880]{1,0:T(8,128)(2,1)} copy(bf16[1024,2880]{0,1:T(8,128)(2,1)} %convolution_convert_fusion.1) | data formatting | bytes 11796480 | tf_op jit(solution)/shard_map/convert_element_type | solution.py:37
  73.8 27.5 %reshape.234 = bf16[1,512,2,16,180]{4,3,2,1,0:T(8,128)(2,1)} reshape(bf16[1024,2880]{1,0:T(8,128)(2,1)} %copy.23) | data formatting | bytes 11796480 | tf_op jit(solution)/shard_map/reshape | solution.py:42
  201.1 11.1 %all-to-all-start = ((bf16[64,1,8,2,16,180]{5,4,3,2,1,0:T(8,128)(2,1)}), bf16[64,1,8,2,16,180]{5,4,3,2,1,0:T(8,128)(2,1)}, u32[]{:S(2)}, u32[]{:S(2)}) async-start(bf16[64,1,8,2,16,180]{5,4,3,2,1,0:T(8,128)(2,1)} %constant_dynamic-update-slice_fusion), calls=%async_computation | async-start | bytes 16777216 | tf_op jit(solution)/shard_map/all_to_all | solution.py:39
  213.1 16.2 %while.1 = (s32[]{:T(128)}, f32[1440,256]{1,0:T(8,128)S(1)}, s32[8,2]{0,1:T(2,128)S(1)}, f32[8,720,256]{2,1,0:T(8,128)}, s32[]{:T(128)}) while((s32[]{:T(128)}, f32[1440,256]{1,0:T(8,128)S(1)}, s32[8,2]{0,1:T(2,128)S(1)}, f32[8,720,256]{2,1,0:T(8,128)}, s32[]{:T(128)}) %tuple.21), condition=%wide.while_cond, body=%wide.while_body.sunk | while | flops 2 | bytes 1475673 | solution.py:64
  229.4 13.0 %mul.158 = f32[8,720,2,256]{3,2,1,0:T(2,128)} broadcast(f32[8,720,256]{2,1,0:T(8,128)} %get-tuple-element.12), dimensions={0,1,3} | broadcast | bytes 17694720 | tf_op jit(solution)/shard_map/mul | solution.py:70
  242.4 14.9 %mul.159 = f32[11520,256]{1,0:T(8,128)} reshape(f32[8,720,2,256]{3,2,1,0:T(2,128)} %mul.158) | data formatting | bytes 23592960 | tf_op jit(solution)/shard_map/mul | solution.py:70
  261.3 72.6 %all-to-all-done = bf16[64,1,8,2,16,180]{5,4,3,2,1,0:T(8,128)(2,1)} async-done(((bf16[64,1,8,2,16,180]{5,4,3,2,1,0:T(8,128)(2,1)}), bf16[64,1,8,2,16,180]{5,4,3,2,1,0:T(8,128)(2,1)}, u32[]{:S(2)}, u32[]{:S(2)}) %all-to-all-start) | async-done | bytes 5898272 | tf_op jit(solution)/shard_map/all_to_all | solution.py:39
  333.9 12.1 %copy.43 = bf16[4,16,8,2,16,180]{5,0,4,1,3,2:T(4,128)(2,1)} copy(bf16[4,16,8,2,16,180]{5,4,3,2,1,0:T(8,128)(2,1)} %bitcast.64) | data formatting | bytes 11796480 | tf_op jit(solution)/shard_map/reshape;reshape | solution.py:53
  346.0 15.3 %reshape.235 = bf16[8,512,720]{2,1,0:T(8,128)(2,1)} reshape(bf16[8,2,16,16,4,180]{5,4,3,2,1,0:T(4,128)(2,1)} %bitcast.289) | data formatting | bytes 11796480 | tf_op jit(solution)/shard_map/reshape | solution.py:56
  361.2 14.4 %convolution_bitcast_fusion = f32[8,720,512]{2,1,0:T(8,128)} fusion(bf16[8,512,720]{2,1,0:T(8,128)(2,1)} %reshape.235, bf16[8,720,720]{2,1,0:T(8,128)(2,1)} %param.7), kind=kOutput, calls=%fused_computation.19 | convolution fusion | flops 4246732800 | bytes 25989120 | tf_op jit(solution)/shard_map/sjl,sxl->sjx/dot_general | solution.py:61
  375.7 13.5 %reshape.236 = f32[11520,256]{1,0:T(8,128)} reshape(f32[8,720,512]{2,1,0:T(8,128)} %convolution_bitcast_fusion) | data formatting | bytes 23592960 | tf_op jit(solution)/shard_map/reshape | solution.py:70
  389.2 13.5 %convolution_convert_fusion = bf16[11520,256]{1,0:T(8,128)(2,1)} fusion(bf16[256,256]{1,0:T(8,128)(2,1)S(1)} %copy-done, f32[11520,256]{1,0:T(8,128)} %reshape.236, f32[11520,256]{1,0:T(8,128)} %mul.159, pred[11520]{0:T(1024)(128)(4,1)S(1)} %broadcast_in_dim.37), kind=kOutput, calls=%fused_computation.12 | convolution fusion | flops 1521745920 | bytes 29633792 | tf_op jit(solution)/shard_map/dot_general | solution.py:74
  402.7 9.7 %reshape.237 = bf16[8,720,512]{2,1,0:T(8,128)(2,1)} reshape(bf16[11520,256]{1,0:T(8,128)(2,1)} %convolution_convert_fusion) | data formatting | bytes 11796480 | tf_op jit(solution)/shard_map/reshape | solution.py:77
  412.3 11.8 %convolution_convert_fusion.2 = bf16[8,512,720]{1,2,0:T(8,128)(2,1)} fusion(bf16[8,720,512]{2,1,0:T(8,128)(2,1)} %reshape.237, bf16[8,720,720]{2,1,0:T(8,128)(2,1)} %param.7), kind=kOutput, calls=%fused_computation.20 | convolution fusion | flops 4249681920 | bytes 20090880 | tf_op jit(solution)/shard_map/sjx,sjl->sxl/dot_general | solution.py:78
  432.6 18.0 %reshape.238 = bf16[8,2,16,16,4,180]{5,4,3,2,1,0:T(4,128)(2,1)} reshape(bf16[8,512,720]{2,1,0:T(8,128)(2,1)} %copy.27) | data formatting | bytes 11796480 | tf_op jit(solution)/shard_map/reshape | solution.py:81
  458.9 9.6 %all-to-all-start.1 = ((bf16[64,8,2,16,180]{4,3,2,1,0:T(8,128)(2,1)}), bf16[64,8,2,16,180]{4,3,2,1,0:T(8,128)(2,1)}, u32[]{:S(2)}, u32[]{:S(2)}) async-start(bf16[64,8,2,16,180]{4,3,2,1,0:T(8,128)(2,1)} %bitcast.291), calls=%async_computation.1 | async-start | bytes 16777216 | tf_op jit(solution)/shard_map/all_to_all | solution.py:85
  479.5 111.9 %all-to-all-done.1 = bf16[64,8,2,16,180]{4,3,2,1,0:T(8,128)(2,1)} async-done(((bf16[64,8,2,16,180]{4,3,2,1,0:T(8,128)(2,1)}), bf16[64,8,2,16,180]{4,3,2,1,0:T(8,128)(2,1)}, u32[]{:S(2)}, u32[]{:S(2)}) %all-to-all-start.1) | async-done | bytes 5898272 | tf_op jit(solution)/shard_map/all_to_all | solution.py:85
  591.4 15.6 %reshape.240 = bf16[1024,2880]{1,0:T(8,128)(2,1)} reshape(bf16[64,8,2,16,180]{4,3,2,1,0:T(8,128)(2,1)} %all-to-all-done.1) | data formatting | bytes 11796480 | tf_op jit(solution)/shard_map/reshape | solution.py:86
  623.4 16.3 %fusion.11 = f32[16,180,1440]{2,1,0:T(8,128)} fusion(bf16[16,180,1024]{2,1,0:T(8,128)(2,1)} %dot_general.27, bf16[1024,1440]{1,0:T(8,128)(2,1)} %convert_element_type.70), kind=kOutput, calls=%fused_computation.21 | convolution fusion | flops 8493465600 | bytes 25436160 | tf_op jit(solution)/shard_map/dot_general | solution.py:87
  639.7 15.3 %fusion.8 = bf16[16,180,1440]{2,0,1:T(8,128)(2,1)} fusion(f32[16,180,1440]{2,1,0:T(8,128)} %fusion.11, bf16[16,180,1440]{2,0,1:T(8,128)(2,1)S(1)} %bitcast.288), kind=kLoop, calls=%fused_computation.11 | loop fusion | flops 45619200 | bytes 33177600 | tf_op jit(solution)/shard_map/convert_element_type | solution.py:94
  (120 shorter events, 179.6 us)
Async XLA Ops:
  0.0 389.2 %copy-start = (bf16[256,256]{1,0:T(8,128)(2,1)S(1)}, bf16[256,256]{1,0:T(8,128)(2,1)}, u32[]{:S(2)}) copy-start(bf16[256,256]{1,0:T(8,128)(2,1)} %param.9) | copy-start | bytes 393220
  40.5 10.9 %copy-start.2 = (bf16[1024,1440]{1,0:T(8,128)(2,1)S(1)}, bf16[1024,1440]{1,0:T(8,128)(2,1)}, u32[]{:S(2)}) copy-start(bf16[1024,1440]{1,0:T(8,128)(2,1)} %convert_element_type.65) | copy-start | bytes 8847364
  201.1 11.9 %copy-start.3 = (f32[720,256]{1,0:T(8,128)S(1)}, f32[720,256]{1,0:T(8,128)}, u32[]{:S(2)}) copy-start(f32[720,256]{1,0:T(8,128)} %param.8) | copy-start | bytes 2211844
  201.1 132.7 %all-to-all-start = ((bf16[64,1,8,2,16,180]{5,4,3,2,1,0:T(8,128)(2,1)}), bf16[64,1,8,2,16,180]{5,4,3,2,1,0:T(8,128)(2,1)}, u32[]{:S(2)}, u32[]{:S(2)}) async-start(bf16[64,1,8,2,16,180]{5,4,3,2,1,0:T(8,128)(2,1)} %constant_dynamic-update-slice_fusion), calls=%async_computation | async-start | bytes 16777216 | tf_op jit(solution)/shard_map/all_to_all | solution.py:39
  458.9 132.5 %all-to-all-start.1 = ((bf16[64,8,2,16,180]{4,3,2,1,0:T(8,128)(2,1)}), bf16[64,8,2,16,180]{4,3,2,1,0:T(8,128)(2,1)}, u32[]{:S(2)}, u32[]{:S(2)}) async-start(bf16[64,8,2,16,180]{4,3,2,1,0:T(8,128)(2,1)} %bitcast.291), calls=%async_computation.1 | async-start | bytes 16777216 | tf_op jit(solution)/shard_map/all_to_all | solution.py:85
  615.4 24.3 %slice-start = ((s8[8847360]{0:T(1024)(128)(4,1)}), s8[458752]{0:T(1024)(128)(4,1)S(1)}, s32[]{:S(2)}) async-start(s8[8847360]{0:T(1024)(128)(4,1)} %bitcast.287), calls=%async_computation.2 | async-start | bytes 917504
  623.4 16.3 %slice-start.1 = ((s8[8847360]{0:T(1024)(128)(4,1)}), s8[4194304]{0:T(1024)(128)(4,1)S(1)}, s32[]{:S(2)}) async-start(s8[8847360]{0:T(1024)(128)(4,1)} %bitcast.287), calls=%async_computation.3 | async-start | bytes 8388608
  623.4 16.3 %slice-start.2 = ((s8[8847360]{0:T(1024)(128)(4,1)}), s8[4194304]{0:T(1024)(128)(4,1)S(1)}, s32[]{:S(2)}) async-start(s8[8847360]{0:T(1024)(128)(4,1)} %bitcast.287), calls=%async_computation.4 | async-start | bytes 8388608
  639.7 15.3 %copy-start.1 = (bf16[256,256]{1,0:T(8,128)(2,1)S(1)}, bf16[256,256]{1,0:T(8,128)(2,1)}, u32[]{:S(2)}) copy-start(bf16[256,256]{1,0:T(8,128)(2,1)} %param.9) | copy-start | bytes 393220
